TPU v7x, 32 devices: a whole 2x2x4 slice. The times are simulated.
32 devices in a mesh: sky: 8 (over y, x, core), tm: 4 (over z).
Axes of the slice: x: 2, y: 2, z: 4, core: 2. Of those that a mesh axis runs over, the one named last changes fastest.
Arguments:
- obs_source: int32 [131072], P(('sky', 'tm')), may hold values from 0 to 1023
- obs_knot: int32 [131072], P(('sky', 'tm')), may hold values from 0 to 2047, as said below
- obs_count: int32 [32], P(('sky', 'tm')), may hold values from 256 to 4096, as said below
- src_design: float32 [5, 131072], P(None, ('sky', 'tm')), may hold values from -3 to 3
- att_design: float32 [4, 131072], P(None, ('sky', 'tm')), may hold values from -6 to 6
- obs_phase: float32 [131072], P(('sky', 'tm')), may hold values from 0 to 1
- obs_value: float32 [131072], P(('sky', 'tm')), may hold values from -6 to 6
- src_prior: float32 [5, 8192], P(None, 'sky'), may hold values from 1 to 16
Outputs:
- att_solution: float32 [4, 4, 2048], P(None, 'tm', 'sky')
- att_residual: float32 [4, 4, 2048], P(None, 'tm', 'sky')
- source_solution: float32 [5, 8192], P(None, 'sky')
Inputs may be any that keep to these rules, and one draw needn't show every extreme that they name: Block b holds the 4096 observation slots o with o // 4096 = b; with i = b // 4 its sources are the sources i * 1024 + obs_source. With j = b % 4 for the observation's block b, its four spline knots are j * 2048 + obs_knot and the next three. In every block, each range of 256 values r * 256 to r * 256 + 255 of obs_knot holds exactly 512 of the block's slots. `obs_count`: each count is 4096 divided by 1, 2, 4, 8 or 16; the live slots of a block are its first ones; some block is full.
All inputs are finite; a program needn't handle non-finite values.
Results may differ from a plain program's by a relative error of at most 0.0001.
Values sent between devices are 32-bit elements; how exact they have to be, the bound alone decides.
A program may use at most 64 MiB of HBM per device.

v0:
```python
import jax
import jax.numpy as jnp
from jax import lax
from jax.sharding import PartitionSpec as P

ITERS = 2
SRC_DEV = 1024
KN_DEV = 256
damping = 0.5
entry_pairs = [(row_at, col_at) for row_at in range(5) for col_at in range(row_at + 1)]


def shifted(value, axis, steps):
    count = lax.axis_size(axis)
    first, last = (max(0, -steps), min(count, count - steps))
    return lax.ppermute(value, axis, [(source, source + steps) for source in range(first, last)])


def spline_taps(phase):
    squared = phase * phase
    cubed = squared * phase
    rest = 1.0 - phase
    return (
        rest * rest * rest / 6.0,
        (3.0 * cubed - 6.0 * squared + 4.0) / 6.0,
        (-3.0 * cubed + 3.0 * squared + 3.0 * phase + 1.0) / 6.0,
        cubed / 6.0,
    )


def factorize(normal):
    factor = {}
    for row_at in range(5):
        for col_at in range(row_at + 1):
            running = normal[row_at, col_at]
            for inner_at in range(col_at):
                running = running - factor[row_at, inner_at] * factor[col_at, inner_at]
            if row_at == col_at:
                factor[row_at, row_at] = jnp.sqrt(running)
            else:
                factor[row_at, col_at] = running / factor[col_at, col_at]
    return factor


def chol_solve(factor, target):
    forward = []
    for row_at in range(5):
        running = target[row_at]
        for inner_at in range(row_at):
            running = running - factor[row_at, inner_at] * forward[inner_at]
        forward.append(running / factor[row_at, row_at])
    result = [None] * 5
    for row_at in reversed(range(5)):
        running = forward[row_at]
        for inner_at in range(row_at + 1, 5):
            running = running - factor[inner_at, row_at] * result[inner_at]
        result[row_at] = running / factor[row_at, row_at]
    return jnp.stack(result)


def source_total(source, rows, count):
    return jnp.zeros((rows.shape[0], count), jnp.float32).at[:, source].add(rows)


def knot_values(padded, knot, design, tap_weights):
    summed = jnp.zeros(knot.shape, jnp.float32)
    for tap_at in range(4):
        picked = jnp.take(padded, knot + tap_at, axis=1)
        summed = summed + tap_weights[tap_at] * jnp.sum(design * picked, axis=0)
    return summed


def knot_total(knot, design, tap_weights, weight_vec, extent):
    summed = jnp.zeros((design.shape[0], extent + 3), jnp.float32)
    for tap_at in range(4):
        summed = summed.at[:, knot + tap_at].add(design * (tap_weights[tap_at] * weight_vec))
    return summed


def eliminate(factor, source, design, values_obs, source_sums):
    solved = chol_solve(factor, [source_sums[row_at] for row_at in range(5)])
    fitted = jnp.sum(design * jnp.take(solved, source, axis=1), axis=0)
    return values_obs - fitted


def shards(
    obs_source, obs_knot, obs_count, src_design, att_design, obs_phase, obs_value, src_prior
):
    sky_count = lax.axis_size("sky")
    seg_knots = KN_DEV * sky_count
    slot_count = obs_source.shape[0]
    live_mask = (jnp.arange(slot_count, dtype=jnp.int32) < obs_count[0]).astype(jnp.float32)
    src_rows = src_design * live_mask
    att_rows = att_design * live_mask
    observed = obs_value * live_mask
    tap_weights = spline_taps(obs_phase)
    products = jnp.stack(
        [src_rows[row_at] * src_rows[col_at] for row_at, col_at in entry_pairs]
        + [src_rows[row_at] * observed for row_at in range(5)]
    )
    sums = lax.psum(source_total(obs_source, products, SRC_DEV), "tm")
    normal = {}
    for entry_at, pair in enumerate(entry_pairs):
        normal[pair] = sums[entry_at] + (src_prior[pair[0]] if pair[0] == pair[1] else 0.0)
    factor = factorize(normal)

    def source_part(values_obs):
        return lax.psum(source_total(obs_source, src_rows * values_obs, SRC_DEV), "tm")

    def along_knots(field):
        segment = lax.all_gather(field, "sky", axis=1, tiled=True)
        next_edge = shifted(segment[:, :3], "tm", -1)
        padded = jnp.concatenate([segment, next_edge], axis=1)
        return knot_values(padded, obs_knot, att_rows, tap_weights)

    def back_to_knots(cleaned):
        summed = knot_total(obs_knot, att_rows, tap_weights, cleaned, seg_knots)
        overflow = shifted(summed[:, seg_knots:], "tm", 1)
        partial_value = summed[:, :seg_knots].at[:, :3].add(overflow)
        return lax.psum_scatter(partial_value, "sky", scatter_dimension=1, tiled=True)

    def norm_sum(partial_value):
        return lax.psum(partial_value, ("sky", "tm"))

    cleaned = eliminate(factor, obs_source, src_rows, observed, sums[15:])
    residual = back_to_knots(cleaned)
    solution = jnp.zeros_like(residual)
    direction = residual
    norm_now = norm_sum(jnp.sum(residual * residual))
    for repeat in range(ITERS):
        image_obs = along_knots(direction)
        cleaned = eliminate(factor, obs_source, src_rows, image_obs, source_part(image_obs))
        mapped = back_to_knots(cleaned) + damping * direction
        alpha_step = norm_now / lax.psum(jnp.sum(direction * mapped), ("sky", "tm"))
        solution = solution + alpha_step * direction
        residual = residual - alpha_step * mapped
        norm_next = norm_sum(jnp.sum(residual * residual))
        direction = residual + norm_next / norm_now * direction
        norm_now = norm_next
    fitted = observed - along_knots(solution)
    source_solution = chol_solve(factor, [row for row in source_part(fitted)])
    return (solution[:, None, :], residual[:, None, :], source_solution)


def solution(mesh):
    placed = (
        P(("sky", "tm")),
        P(("sky", "tm")),
        P(("sky", "tm")),
        P(None, ("sky", "tm")),
        P(None, ("sky", "tm")),
        P(("sky", "tm")),
        P(("sky", "tm")),
        P(None, "sky"),
    )
    return jax.shard_map(
        shards,
        mesh=mesh,
        in_specs=placed,
        out_specs=(P(None, "tm", "sky"), P(None, "tm", "sky"), P(None, "sky")),
        check_vma=False,
    )
```

profile of v0, /device:TPU:0, one launch (start us, length us, event | category | flops | bytes accessed | tf_op | source)
XLA Modules:
  0.0 1068.1 jit_solution(9590675632088410657)
XLA Ops:
  11.7 22.5 %scatter_custom_fusion = f32[20,1024]{0,1:T(8,128)S(1)} fusion(s32[4096]{0:T(1024)S(1)} %get-tuple-element.173, f32[4096,20]{1,0:T(8,128)S(1)} %copy.271, f32[]{:T(128)} %constant.111.clone.1), kind=kCustom, calls=%fused_computation.113 | custom fusion | flops 81920 | bytes 81924 | tf_op jit(solution)/shard_map/scatter-add | solution.py:62
  37.1 35.3 %all-reduce.3.cloned.1.call-done = f32[20,1024]{1,0:T(8,128)} async-done(((f32[20,1024]{1,0:T(8,128)}), f32[20,1024]{1,0:T(8,128)}) %all-reduce.3.cloned.1.call-update) | async-done | bytes 81936 | tf_op jit(solution)/shard_map/psum | solution.py:101
  75.5 14.1 %gather_fusion = f32[4096,5]{1,0:T(8,128)} fusion(f32[5,1024]{0,1:T(8,128)S(1)} %copy.273, s32[4096]{0:T(1024)S(1)} %get-tuple-element.172), kind=kCustom, calls=%fused_computation.clone | custom fusion | bytes 180224 | tf_op jit(solution)/shard_map/jit(_take)/gather | solution.py:82
  92.0 25.3 %scatter_custom_fusion.1 = f32[4,2051]{0,1:T(8,128)S(1)} fusion(s32[4096]{0:T(1024)} %get-tuple-element.168, f32[4096]{0:T(1024)S(1)} %get-tuple-element.159, f32[]{:T(128)} %constant.111.clone.1, f32[4,4096]{0,1:T(8,128)S(1)} %copy.270, f32[4096]{0:T(1024)S(1)} %fusion.83), kind=kCustom, calls=%fused_computation.77 | custom fusion | flops 49152 | bytes 131632 | tf_op jit(solution)/shard_map/scatter-add | solution.py:76
  117.3 25.4 %scatter_custom_fusion.2 = f32[4,2051]{0,1:T(8,128)S(1)} fusion(f32[4,2051]{0,1:T(8,128)S(1)} %scatter_custom_fusion.1, s32[4096]{0:T(1024)} %get-tuple-element.166, f32[4096]{0:T(1024)S(1)} %get-tuple-element.158, f32[4,4096]{0,1:T(8,128)S(1)} %copy.270, f32[4096]{0:T(1024)S(1)} %fusion.83), kind=kCustom, calls=%fused_computation.75 | custom fusion | flops 49152 | bytes 2162736 | tf_op jit(solution)/shard_map/scatter-add | solution.py:76
  142.6 25.4 %scatter_custom_fusion.3 = f32[4,2051]{0,1:T(8,128)S(1)} fusion(f32[4,2051]{0,1:T(8,128)S(1)} %scatter_custom_fusion.2, s32[4096]{0:T(1024)} %get-tuple-element.167, f32[4096]{0:T(1024)S(1)} %get-tuple-element.157, f32[4,4096]{0,1:T(8,128)S(1)} %copy.270, f32[4096]{0:T(1024)S(1)} %fusion.83), kind=kCustom, calls=%fused_computation.73 | custom fusion | flops 49152 | bytes 2162736 | tf_op jit(solution)/shard_map/scatter-add | solution.py:76
  168.1 25.4 %scatter_custom_fusion.4 = f32[4,2051]{0,1:T(8,128)S(1)} fusion(f32[4,2051]{0,1:T(8,128)S(1)} %scatter_custom_fusion.3, s32[4096]{0:T(1024)S(1)} %get-tuple-element.171, f32[4096]{0:T(1024)S(1)} %get-tuple-element.106, f32[4,4096]{0,1:T(8,128)S(1)} %copy.270, f32[4096]{0:T(1024)S(1)} %fusion.83), kind=kCustom, calls=%fused_computation.71 | custom fusion | flops 49152 | bytes 2162736 | tf_op jit(solution)/shard_map/scatter-add | solution.py:76
  201.3 36.5 %reduce-scatter.10.cloned.1.call-done = f32[256,4]{1,0:T(8,128)} async-done(((f32[2048,4]{1,0:T(8,128)}), f32[256,4]{1,0:T(8,128)}) %reduce-scatter.10.cloned.1.call-update) | async-done | bytes 4112
  282.5 14.1 %gather_fusion.2 = f32[4096,4]{1,0:T(8,128)} fusion(f32[4,2051]{0,1:T(8,128)S(1)} %constant_dynamic-update-slice_fusion, s32[4096]{0:T(1024)S(1)} %get-tuple-element.170), kind=kCustom, calls=%fused_computation.4.clone | custom fusion | bytes 147456 | tf_op jit(solution)/shard_map/jit(_take)/gather | solution.py:68
  321.7 22.8 %scatter_custom_fusion.5 = f32[5,1024]{0,1:T(8,128)S(1)} fusion(s32[4096]{0:T(1024)} %copy-done.35, f32[4096,5]{1,0:T(8,128)} %copy.277, f32[]{:T(128)} %constant.111.clone.1), kind=kCustom, calls=%fused_computation.111 | custom fusion | flops 20480 | bytes 20992 | tf_op jit(solution)/shard_map/scatter-add | solution.py:62
  344.6 17.2 %psum.58 = f32[5,1024]{1,0:T(8,128)S(1)} all-reduce(f32[5,1024]{1,0:T(8,128)S(1)} %copy.278), channel_id=1, replica_groups=mesh['sky'=8,'tm'=4] {'tm'}, use_global_device_ids=true, to_apply=%region_16.19 | all-reduce | flops 5120 | bytes 40960 | tf_op jit(solution)/shard_map/psum | solution.py:108
  363.1 14.1 %gather_fusion.5 = f32[4096,5]{1,0:T(8,128)} fusion(f32[5,1024]{0,1:T(8,128)S(1)} %copy.279, s32[4096]{0:T(1024)S(1)} %get-tuple-element.172), kind=kCustom, calls=%fused_computation.2.clone | custom fusion | bytes 180224 | tf_op jit(solution)/shard_map/jit(_take)/gather | solution.py:82
  379.6 25.3 %scatter_custom_fusion.6 = f32[4,2051]{0,1:T(8,128)S(1)} fusion(s32[4096]{0:T(1024)} %get-tuple-element.168, f32[4096]{0:T(1024)S(1)} %get-tuple-element.156, f32[]{:T(128)} %constant.111.clone.1, f32[4,4096]{0,1:T(8,128)S(1)} %copy.270, f32[4096]{0:T(1024)S(1)} %fusion.83), kind=kCustom, calls=%fused_computation.61 | custom fusion | flops 49152 | bytes 131632 | tf_op jit(solution)/shard_map/scatter-add | solution.py:76
  404.8 25.6 %scatter_custom_fusion.7 = f32[4,2051]{0,1:T(8,128)S(1)} fusion(f32[4,2051]{0,1:T(8,128)S(1)} %scatter_custom_fusion.6, s32[4096]{0:T(1024)} %get-tuple-element.166, f32[4096]{0:T(1024)S(1)} %get-tuple-element.155, f32[4,4096]{0,1:T(8,128)S(1)} %copy.270, f32[4096]{0:T(1024)S(1)} %fusion.83), kind=kCustom, calls=%fused_computation.59 | custom fusion | flops 49152 | bytes 2162736 | tf_op jit(solution)/shard_map/scatter-add | solution.py:76
  430.5 25.4 %scatter_custom_fusion.8 = f32[4,2051]{0,1:T(8,128)S(1)} fusion(f32[4,2051]{0,1:T(8,128)S(1)} %scatter_custom_fusion.7, s32[4096]{0:T(1024)} %get-tuple-element.167, f32[4096]{0:T(1024)S(1)} %get-tuple-element.154, f32[4,4096]{0,1:T(8,128)S(1)} %copy.270, f32[4096]{0:T(1024)S(1)} %fusion.83), kind=kCustom, calls=%fused_computation.57 | custom fusion | flops 49152 | bytes 2162736 | tf_op jit(solution)/shard_map/scatter-add | solution.py:76
  455.8 25.4 %scatter_custom_fusion.9 = f32[4,2051]{0,1:T(8,128)S(1)} fusion(f32[4,2051]{0,1:T(8,128)S(1)} %scatter_custom_fusion.8, s32[4096]{0:T(1024)} %copy-done.36, f32[4096]{0:T(1024)S(1)} %get-tuple-element.95, f32[4,4096]{0,1:T(8,128)S(1)} %copy.270, f32[4096]{0:T(1024)S(1)} %fusion.83), kind=kCustom, calls=%fused_computation.55 | custom fusion | flops 49152 | bytes 2162736 | tf_op jit(solution)/shard_map/scatter-add | solution.py:76
  487.6 36.2 %reduce-scatter.12.cloned.1.call-done = f32[256,4]{1,0:T(8,128)} async-done(((f32[2048,4]{1,0:T(8,128)}), f32[256,4]{1,0:T(8,128)}) %reduce-scatter.12.cloned.1.call-update) | async-done | bytes 4112
  525.4 39.5 %all-reduce = (f32[]{:T(128)}, f32[]{:T(128)}) all-reduce(f32[]{:T(128)} %get-tuple-element.72, f32[]{:T(128)} %get-tuple-element.71), channel_id=1, replica_groups=mesh['sky'=8,'tm'=4] {'sky','tm'}, use_global_device_ids=true, to_apply=%region_10.12 | all-reduce | flops 2 | bytes 16 | tf_op jit(solution)/shard_map/psum | solution.py:123
  566.7 41.3 %psum.60 = f32[]{:T(128)} all-reduce(f32[]{:T(128)} %multiply_reduce_fusion.1), channel_id=1, replica_groups=mesh['sky'=8,'tm'=4] {'sky','tm'}, use_global_device_ids=true, to_apply=%region_26.29 | all-reduce | flops 1 | bytes 8 | tf_op jit(solution)/shard_map/psum | solution.py:123
  653.3 14.1 %gather_fusion.7 = f32[4096,4]{1,0:T(8,128)} fusion(f32[4,2051]{0,1:T(8,128)S(1)} %copy.282, s32[4096]{0:T(1024)S(1)} %get-tuple-element.170), kind=kCustom, calls=%fused_computation.8.clone | custom fusion | bytes 147456 | tf_op jit(solution)/shard_map/jit(_take)/gather | solution.py:68
  693.1 22.8 %scatter_custom_fusion.10 = f32[5,1024]{0,1:T(8,128)S(1)} fusion(s32[4096]{0:T(1024)} %copy-done.35, f32[4096,5]{1,0:T(8,128)} %copy.286, f32[]{:T(128)} %constant.111.clone.1), kind=kCustom, calls=%fused_computation.109 | custom fusion | flops 20480 | bytes 20992 | tf_op jit(solution)/shard_map/scatter-add | solution.py:62
  716.1 16.2 %psum.61 = f32[5,1024]{1,0:T(8,128)S(1)} all-reduce(f32[5,1024]{1,0:T(8,128)S(1)} %copy.287), channel_id=1, replica_groups=mesh['sky'=8,'tm'=4] {'tm'}, use_global_device_ids=true, to_apply=%region_32.35 | all-reduce | flops 5120 | bytes 40960 | tf_op jit(solution)/shard_map/psum | solution.py:108
  733.6 14.1 %gather_fusion.10 = f32[4096,5]{1,0:T(8,128)} fusion(f32[5,1024]{0,1:T(8,128)S(1)} %copy.288, s32[4096]{0:T(1024)S(1)} %get-tuple-element.172), kind=kCustom, calls=%fused_computation.3.clone | custom fusion | bytes 180224 | tf_op jit(solution)/shard_map/jit(_take)/gather | solution.py:82
  750.0 25.3 %scatter_custom_fusion.11 = f32[4,2051]{0,1:T(8,128)S(1)} fusion(s32[4096]{0:T(1024)} %get-tuple-element.168, f32[4096]{0:T(1024)S(1)} %get-tuple-element.153, f32[]{:T(128)} %constant.111.clone.1, f32[4,4096]{0,1:T(8,128)S(1)} %copy.270, f32[4096]{0:T(1024)S(1)} %fusion.83), kind=kCustom, calls=%fused_computation.45 | custom fusion | flops 49152 | bytes 131632 | tf_op jit(solution)/shard_map/scatter-add | solution.py:76
  775.3 25.4 %scatter_custom_fusion.12 = f32[4,2051]{0,1:T(8,128)S(1)} fusion(f32[4,2051]{0,1:T(8,128)S(1)} %scatter_custom_fusion.11, s32[4096]{0:T(1024)} %get-tuple-element.166, f32[4096]{0:T(1024)S(1)} %get-tuple-element.152, f32[4,4096]{0,1:T(8,128)S(1)} %copy.270, f32[4096]{0:T(1024)S(1)} %fusion.83), kind=kCustom, calls=%fused_computation.43 | custom fusion | flops 49152 | bytes 2162736 | tf_op jit(solution)/shard_map/scatter-add | solution.py:76
  800.7 25.4 %scatter_custom_fusion.13 = f32[4,2051]{0,1:T(8,128)S(1)} fusion(f32[4,2051]{0,1:T(8,128)S(1)} %scatter_custom_fusion.12, s32[4096]{0:T(1024)} %get-tuple-element.167, f32[4096]{0:T(1024)S(1)} %get-tuple-element.151, f32[4,4096]{0,1:T(8,128)S(1)} %copy.270, f32[4096]{0:T(1024)S(1)} %fusion.83), kind=kCustom, calls=%fused_computation.41 | custom fusion | flops 49152 | bytes 2162736 | tf_op jit(solution)/shard_map/scatter-add | solution.py:76
  826.1 25.6 %scatter_custom_fusion.14 = f32[4,2051]{0,1:T(8,128)S(1)} fusion(f32[4,2051]{0,1:T(8,128)S(1)} %scatter_custom_fusion.13, s32[4096]{0:T(1024)} %copy-done.36, f32[4096]{0:T(1024)S(1)} %get-tuple-element.84, f32[4,4096]{0,1:T(8,128)S(1)} %copy.270, f32[4096]{0:T(1024)S(1)} %fusion.83), kind=kCustom, calls=%fused_computation.39 | custom fusion | flops 49152 | bytes 2162736 | tf_op jit(solution)/shard_map/scatter-add | solution.py:76
  857.5 36.8 %reduce-scatter.14.cloned.1.call-done = f32[256,4]{1,0:T(8,128)} async-done(((f32[2048,4]{1,0:T(8,128)}), f32[256,4]{1,0:T(8,128)}) %reduce-scatter.14.cloned.1.call-update) | async-done | bytes 4112
  896.0 39.4 %psum.62 = f32[]{:T(128)} all-reduce(f32[]{:T(128)} %multiply_reduce_fusion), channel_id=1, replica_groups=mesh['sky'=8,'tm'=4] {'sky','tm'}, use_global_device_ids=true, to_apply=%region_40.43 | all-reduce | flops 1 | bytes 8 | tf_op jit(solution)/shard_map/psum | solution.py:134
  982.0 14.1 %gather_fusion.12 = f32[4096,4]{1,0:T(8,128)} fusion(f32[4,2051]{0,1:T(8,128)S(1)} %copy.291, s32[4096]{0:T(1024)S(1)} %get-tuple-element.170), kind=kCustom, calls=%fused_computation.12.clone | custom fusion | bytes 147456 | tf_op jit(solution)/shard_map/jit(_take)/gather | solution.py:68
  1019.8 22.6 %scatter_custom_fusion.15 = f32[5,1024]{0,1:T(8,128)S(1)} fusion(s32[4096]{0:T(1024)} %copy-done.35, f32[4096,5]{1,0:T(8,128)S(1)} %copy.295, f32[]{:T(128)} %constant.111.clone.1), kind=kCustom, calls=%fused_computation.107 | custom fusion | flops 20480 | bytes 20992 | tf_op jit(solution)/shard_map/scatter-add | solution.py:62
  1042.6 17.2 %psum.63 = f32[5,1024]{1,0:T(8,128)S(1)} all-reduce(f32[5,1024]{1,0:T(8,128)S(1)} %copy.296), channel_id=1, replica_groups=mesh['sky'=8,'tm'=4] {'tm'}, use_global_device_ids=true, to_apply=%region_46.49 | all-reduce | flops 5120 | bytes 40960 | tf_op jit(solution)/shard_map/psum | solution.py:108
  (193 shorter events, 253.3 us)
Async XLA Ops:
  7.2 65.2 %all-reduce.3.cloned.1.call-start = ((), (), s32[]{:S(2)}) async-start(), calls=%async_computation.3 | async-start | bytes 196608 | tf_op jit(solution)/shard_map/psum | solution.py:101
  11.7 60.7 %copy-start.34 = (f32[5,1024]{1,0:T(8,128)S(1)}, f32[5,1024]{1,0:T(8,128)}, u32[]{:S(2)}) copy-start(f32[5,1024]{1,0:T(8,128)} %param.25) | copy-start | bytes 61444
  35.0 202.8 %reduce-scatter.10.cloned.1.call-start = ((), (), s32[]{:S(2)}) async-start(), calls=%async_computation.4 | async-start | bytes 1179648
  35.7 132.3 %copy-start.36 = (s32[4096]{0:T(1024)}, s32[4096]{0:T(1024)S(1)}, u32[]{:S(2)}) copy-start(s32[4096]{0:T(1024)S(1)} %get-tuple-element.171) | copy-start | bytes 49156
  35.7 343.7 %copy-start.21 = (pred[4096]{0:T(1024)(128)(4,1)}, pred[4096]{0:T(1024)(128)(4,1)S(1)}, u32[]{:S(2)}) copy-start(pred[4096]{0:T(1024)(128)(4,1)S(1)} %compare_and_fusion.4) | copy-start | bytes 12292
  73.6 288.4 %copy-start.3 = (f32[1,1024]{1,0:T(1,128)}, f32[1,1024]{1,0:T(1,128)S(1)}, u32[]{:S(2)}) copy-start(f32[1,1024]{1,0:T(1,128)S(1)} %get-tuple-element.128) | copy-start | bytes 12292
  73.6 288.4 %copy-start.5 = (f32[1,1024]{1,0:T(1,128)}, f32[1,1024]{1,0:T(1,128)S(1)}, u32[]{:S(2)}) copy-start(f32[1,1024]{1,0:T(1,128)S(1)} %get-tuple-element.129) | copy-start | bytes 12292
  73.6 288.4 %copy-start.7 = (f32[1,1024]{1,0:T(1,128)}, f32[1,1024]{1,0:T(1,128)S(1)}, u32[]{:S(2)}) copy-start(f32[1,1024]{1,0:T(1,128)S(1)} %get-tuple-element.130) | copy-start | bytes 12292
  194.6 4.6 collective-permute-start
  201.2 322.6 %reduce-scatter.12.cloned.1.call-start = ((), (), s32[]{:S(2)}) async-start(), calls=%async_computation.5 | async-start | bytes 1179648
  201.3 109.3 %copy-start.13 = (pred[4096]{0:T(1024)(128)(4,1)}, pred[4096]{0:T(1024)(128)(4,1)S(1)}, u32[]{:S(2)}) copy-start(pred[4096]{0:T(1024)(128)(4,1)S(1)} %get-tuple-element.160) | copy-start | bytes 12292
  201.3 109.3 %copy-start.15 = (pred[4096]{0:T(1024)(128)(4,1)}, pred[4096]{0:T(1024)(128)(4,1)S(1)}, u32[]{:S(2)}) copy-start(pred[4096]{0:T(1024)(128)(4,1)S(1)} %get-tuple-element.161) | copy-start | bytes 12292
  201.3 109.3 %copy-start.17 = (pred[4096]{0:T(1024)(128)(4,1)}, pred[4096]{0:T(1024)(128)(4,1)S(1)}, u32[]{:S(2)}) copy-start(pred[4096]{0:T(1024)(128)(4,1)S(1)} %get-tuple-element.162) | copy-start | bytes 12292
  201.3 109.3 %copy-start.19 = (pred[4096]{0:T(1024)(128)(4,1)}, pred[4096]{0:T(1024)(128)(4,1)S(1)}, u32[]{:S(2)}) copy-start(pred[4096]{0:T(1024)(128)(4,1)S(1)} %get-tuple-element.163) | copy-start | bytes 12292
  248.8 5.5 collective-permute-start.1
  319.6 42.4 %copy-start.26 = (f32[1,1024]{1,0:T(1,128)S(1)}, f32[1,1024]{1,0:T(1,128)}, u32[]{:S(2)}) copy-start(f32[1,1024]{1,0:T(1,128)} %get-tuple-element.113) | copy-start | bytes 12292
  319.6 42.4 %copy-start.28 = (f32[1,1024]{1,0:T(1,128)S(1)}, f32[1,1024]{1,0:T(1,128)}, u32[]{:S(2)}) copy-start(f32[1,1024]{1,0:T(1,128)} %get-tuple-element.114) | copy-start | bytes 12292
  319.6 42.4 %copy-start.30 = (f32[1,1024]{1,0:T(1,128)S(1)}, f32[1,1024]{1,0:T(1,128)}, u32[]{:S(2)}) copy-start(f32[1,1024]{1,0:T(1,128)} %get-tuple-element.115) | copy-start | bytes 12292
  319.6 42.4 %copy-start.32 = (f32[1,1024]{1,0:T(1,128)S(1)}, f32[1,1024]{1,0:T(1,128)}, u32[]{:S(2)}) copy-start(f32[1,1024]{1,0:T(1,128)} %get-tuple-element.116) | copy-start | bytes 12292
  482.3 2.6 collective-permute-start.2
  487.5 406.9 %reduce-scatter.14.cloned.1.call-start = ((), (), s32[]{:S(2)}) async-start(), calls=%async_computation.6 | async-start | bytes 1179648
  487.6 137.1 %copy-start.11 = (f32[4,256]{1,0:T(4,128)}, f32[4,256]{1,0:T(4,128)S(1)}, u32[]{:S(2)}) copy-start(f32[4,256]{1,0:T(4,128)S(1)} %copy.300) | copy-start | bytes 12292
  619.3 5.5 collective-permute-start.3
  691.0 41.4 %copy-start.27 = (f32[1,1024]{1,0:T(1,128)S(1)}, f32[1,1024]{1,0:T(1,128)}, u32[]{:S(2)}) copy-start(f32[1,1024]{1,0:T(1,128)} %get-tuple-element.113) | copy-start | bytes 12292
  691.0 41.4 %copy-start.29 = (f32[1,1024]{1,0:T(1,128)S(1)}, f32[1,1024]{1,0:T(1,128)}, u32[]{:S(2)}) copy-start(f32[1,1024]{1,0:T(1,128)} %get-tuple-element.114) | copy-start | bytes 12292
  851.6 85.0 %copy-start.12 = (f32[4,256]{1,0:T(4,128)S(1)}, f32[4,256]{1,0:T(4,128)}, u32[]{:S(2)}) copy-start(f32[4,256]{1,0:T(4,128)} %copy-done.11) | copy-start | bytes 12292
  852.7 2.8 collective-permute-start.4
  857.5 152.6 %copy-start.14 = (pred[4096]{0:T(1024)(128)(4,1)S(1)}, pred[4096]{0:T(1024)(128)(4,1)}, u32[]{:S(2)}) copy-start(pred[4096]{0:T(1024)(128)(4,1)} %copy-done.13) | copy-start | bytes 12292
  857.5 152.6 %copy-start.16 = (pred[4096]{0:T(1024)(128)(4,1)S(1)}, pred[4096]{0:T(1024)(128)(4,1)}, u32[]{:S(2)}) copy-start(pred[4096]{0:T(1024)(128)(4,1)} %copy-done.15) | copy-start | bytes 12292
  857.5 152.6 %copy-start.18 = (pred[4096]{0:T(1024)(128)(4,1)S(1)}, pred[4096]{0:T(1024)(128)(4,1)}, u32[]{:S(2)}) copy-start(pred[4096]{0:T(1024)(128)(4,1)} %copy-done.17) | copy-start | bytes 12292
  857.5 152.6 %copy-start.20 = (pred[4096]{0:T(1024)(128)(4,1)S(1)}, pred[4096]{0:T(1024)(128)(4,1)}, u32[]{:S(2)}) copy-start(pred[4096]{0:T(1024)(128)(4,1)} %copy-done.19) | copy-start | bytes 12292
  948.0 5.5 collective-permute-start.5
  (15 other events, 390.2 us)
Sparse Core Ops, SparseCore 0:
  35.1 37.1 all-reduce.2
  201.3 36.4 reduce-scatter.9
  487.6 36.1 reduce-scatter.11
  857.6 36.7 reduce-scatter.13
where the time goes:
time: 1080 us; the launch traced here: 1070 us
  other arithmetic  437 us (40%)
  local copies, waits for them, and re-layouts  238 us (22%)
  blocking collectives  202 us (19%)
  waiting for transfers between devices  161 us (15%)
  between operations  19.3 us (2%)
    scatter-add x12, other arithmetic, knot_total(): summed.at[:, knot + tap_at].add(design * (tap_weights[tap_at] * weight_vec))  305 us
    gather x12, local copies, waits for them, and re-layouts, knot_values(): picked = jnp.take(padded, knot + tap_at, axis=1)  169 us
    unnamed x7, waiting for transfers between devices  110 us
    scatter-add x4, other arithmetic, source_total(): jnp.zeros((rows.shape[0], count), jnp.float32).at[:, source].add(rows)  90.6 us
    psum x2, blocking collectives, norm_sum(): return lax.psum(partial_value, ('sky', 'tm'))  80.7 us
    psum x3, blocking collectives, source_part(): lax.psum(source_total(obs_source, src_rows * values_obs, SRC_DEV), 'tm')  50.7 us
    gather x6, local copies, waits for them, and re-layouts, eliminate(): fitted = jnp.sum(design * jnp.take(solved, source, axis=1), axis=0)  48.9 us
    psum x1, blocking collectives, shards(): alpha_step = norm_now / lax.psum(jnp.sum(direction * mapped), ('sky', 'tm'))  39.4 us
  transfers between devices with their start and end apart: 10, of which 10 were waited for; matrix products, arithmetic and copies ran while one was open for 0% of the time, Pallas kernels for 0%

commit v1 on v0

--- a/solution.py
+++ b/solution.py
@@ -120,7 +120,7 @@
         return lax.psum_scatter(partial_value, "sky", scatter_dimension=1, tiled=True)
 
     def norm_sum(partial_value):
-        return lax.psum(partial_value, ("sky", "tm"))
+        return lax.psum(lax.psum(partial_value, "sky"), "tm")
 
     cleaned = eliminate(factor, obs_source, src_rows, observed, sums[15:])
     residual = back_to_knots(cleaned)

time: 1080 us -> 1080 us (level)
    psum x1 -> x2, blocking collectives: 39.4 us -> 76.4 us  [shards(): alpha_step = norm_now / lax.psum(jnp.sum(direction * mapped), ('sky', 'tm'))]
    psum x2 -> x4, blocking collectives: 80.7 us -> 50.6 us  [norm_sum(): return lax.psum(lax.psum(partial_value, 'sky'), 'tm')]
where the time goes in v1:
time: 1080 us; the launch traced here: 1070 us
  other arithmetic  437 us (40%)
  local copies, waits for them, and re-layouts  238 us (22%)
  blocking collectives  207 us (19%)
  waiting for transfers between devices  161 us (15%)
  between operations  19.5 us (2%)
  starting transfers between devices  10.9 us (1%)
    scatter-add x12, other arithmetic, knot_total(): summed.at[:, knot + tap_at].add(design * (tap_weights[tap_at] * weight_vec))  305 us
    gather x12, local copies, waits for them, and re-layouts, knot_values(): picked = jnp.take(padded, knot + tap_at, axis=1)  169 us
    unnamed x7, waiting for transfers between devices  110 us
    scatter-add x4, other arithmetic, source_total(): jnp.zeros((rows.shape[0], count), jnp.float32).at[:, source].add(rows)  90.6 us
    psum x2, blocking collectives, shards(): alpha_step = norm_now / lax.psum(jnp.sum(direction * mapped), ('sky', 'tm'))  76.4 us
    psum x4, blocking collectives, norm_sum(): return lax.psum(lax.psum(partial_value, 'sky'), 'tm')  50.6 us
    psum x3, blocking collectives, source_part(): lax.psum(source_total(obs_source, src_rows * values_obs, SRC_DEV), 'tm')  50.2 us
    gather x6, local copies, waits for them, and re-layouts, eliminate(): fitted = jnp.sum(design * jnp.take(solved, source, axis=1), axis=0)  48.9 us
  transfers between devices with their start and end apart: 10, of which 10 were waited for; matrix products, arithmetic and copies ran while one was open for 0% of the time, Pallas kernels for 0%

profile of v1, /device:TPU:0, one launch (start us, length us, event | category | flops | bytes accessed | tf_op | source)
XLA Modules:
  0.0 1074.0 jit_solution(11422513508396761795)
XLA Ops:
  11.7 22.5 %scatter_custom_fusion = f32[20,1024]{0,1:T(8,128)S(1)} fusion(s32[4096]{0:T(1024)S(1)} %get-tuple-element.171, f32[4096,20]{1,0:T(8,128)S(1)} %copy.271, f32[]{:T(128)} %constant.111.clone.1), kind=kCustom, calls=%fused_computation.113 | custom fusion | flops 81920 | bytes 81924 | tf_op jit(solution)/shard_map/scatter-add | solution.py:62
  37.1 35.3 %all-reduce.2.cloned.1.call-done = f32[20,1024]{1,0:T(8,128)} async-done(((f32[20,1024]{1,0:T(8,128)}), f32[20,1024]{1,0:T(8,128)}) %all-reduce.2.cloned.1.call-update) | async-done | bytes 81936 | tf_op jit(solution)/shard_map/psum | solution.py:101
  75.5 14.1 %gather_fusion = f32[4096,5]{1,0:T(8,128)} fusion(f32[5,1024]{0,1:T(8,128)S(1)} %copy.273, s32[4096]{0:T(1024)S(1)} %get-tuple-element.170), kind=kCustom, calls=%fused_computation.clone | custom fusion | bytes 180224 | tf_op jit(solution)/shard_map/jit(_take)/gather | solution.py:82
  92.0 25.3 %scatter_custom_fusion.1 = f32[4,2051]{0,1:T(8,128)S(1)} fusion(s32[4096]{0:T(1024)} %get-tuple-element.166, f32[4096]{0:T(1024)S(1)} %get-tuple-element.157, f32[]{:T(128)} %constant.111.clone.1, f32[4,4096]{0,1:T(8,128)S(1)} %copy.270, f32[4096]{0:T(1024)S(1)} %fusion.83), kind=kCustom, calls=%fused_computation.77 | custom fusion | flops 49152 | bytes 131632 | tf_op jit(solution)/shard_map/scatter-add | solution.py:76
  117.3 25.4 %scatter_custom_fusion.2 = f32[4,2051]{0,1:T(8,128)S(1)} fusion(f32[4,2051]{0,1:T(8,128)S(1)} %scatter_custom_fusion.1, s32[4096]{0:T(1024)} %get-tuple-element.164, f32[4096]{0:T(1024)S(1)} %get-tuple-element.156, f32[4,4096]{0,1:T(8,128)S(1)} %copy.270, f32[4096]{0:T(1024)S(1)} %fusion.83), kind=kCustom, calls=%fused_computation.75 | custom fusion | flops 49152 | bytes 2162736 | tf_op jit(solution)/shard_map/scatter-add | solution.py:76
  142.6 25.4 %scatter_custom_fusion.3 = f32[4,2051]{0,1:T(8,128)S(1)} fusion(f32[4,2051]{0,1:T(8,128)S(1)} %scatter_custom_fusion.2, s32[4096]{0:T(1024)} %get-tuple-element.165, f32[4096]{0:T(1024)S(1)} %get-tuple-element.155, f32[4,4096]{0,1:T(8,128)S(1)} %copy.270, f32[4096]{0:T(1024)S(1)} %fusion.83), kind=kCustom, calls=%fused_computation.73 | custom fusion | flops 49152 | bytes 2162736 | tf_op jit(solution)/shard_map/scatter-add | solution.py:76
  168.1 25.4 %scatter_custom_fusion.4 = f32[4,2051]{0,1:T(8,128)S(1)} fusion(f32[4,2051]{0,1:T(8,128)S(1)} %scatter_custom_fusion.3, s32[4096]{0:T(1024)S(1)} %get-tuple-element.169, f32[4096]{0:T(1024)S(1)} %get-tuple-element.104, f32[4,4096]{0,1:T(8,128)S(1)} %copy.270, f32[4096]{0:T(1024)S(1)} %fusion.83), kind=kCustom, calls=%fused_computation.71 | custom fusion | flops 49152 | bytes 2162736 | tf_op jit(solution)/shard_map/scatter-add | solution.py:76
  201.3 36.5 %reduce-scatter.10.cloned.1.call-done = f32[256,4]{1,0:T(8,128)} async-done(((f32[2048,4]{1,0:T(8,128)}), f32[256,4]{1,0:T(8,128)}) %reduce-scatter.10.cloned.1.call-update) | async-done | bytes 4112
  282.5 14.1 %gather_fusion.2 = f32[4096,4]{1,0:T(8,128)} fusion(f32[4,2051]{0,1:T(8,128)S(1)} %constant_dynamic-update-slice_fusion, s32[4096]{0:T(1024)S(1)} %get-tuple-element.168), kind=kCustom, calls=%fused_computation.4.clone | custom fusion | bytes 147456 | tf_op jit(solution)/shard_map/jit(_take)/gather | solution.py:68
  321.7 22.8 %scatter_custom_fusion.5 = f32[5,1024]{0,1:T(8,128)S(1)} fusion(s32[4096]{0:T(1024)} %copy-done.35, f32[4096,5]{1,0:T(8,128)} %copy.277, f32[]{:T(128)} %constant.111.clone.1), kind=kCustom, calls=%fused_computation.111 | custom fusion | flops 20480 | bytes 20992 | tf_op jit(solution)/shard_map/scatter-add | solution.py:62
  344.6 17.2 %psum.73 = f32[5,1024]{1,0:T(8,128)S(1)} all-reduce(f32[5,1024]{1,0:T(8,128)S(1)} %copy.278), channel_id=1, replica_groups=mesh['sky'=8,'tm'=4] {'tm'}, use_global_device_ids=true, to_apply=%region_17.20 | all-reduce | flops 5120 | bytes 40960 | tf_op jit(solution)/shard_map/psum | solution.py:108
  363.1 14.1 %gather_fusion.5 = f32[4096,5]{1,0:T(8,128)} fusion(f32[5,1024]{0,1:T(8,128)S(1)} %copy.279, s32[4096]{0:T(1024)S(1)} %get-tuple-element.170), kind=kCustom, calls=%fused_computation.2.clone | custom fusion | bytes 180224 | tf_op jit(solution)/shard_map/jit(_take)/gather | solution.py:82
  379.6 25.3 %scatter_custom_fusion.6 = f32[4,2051]{0,1:T(8,128)S(1)} fusion(s32[4096]{0:T(1024)} %get-tuple-element.166, f32[4096]{0:T(1024)S(1)} %get-tuple-element.154, f32[]{:T(128)} %constant.111.clone.1, f32[4,4096]{0,1:T(8,128)S(1)} %copy.270, f32[4096]{0:T(1024)S(1)} %fusion.83), kind=kCustom, calls=%fused_computation.61 | custom fusion | flops 49152 | bytes 131632 | tf_op jit(solution)/shard_map/scatter-add | solution.py:76
  404.8 25.6 %scatter_custom_fusion.7 = f32[4,2051]{0,1:T(8,128)S(1)} fusion(f32[4,2051]{0,1:T(8,128)S(1)} %scatter_custom_fusion.6, s32[4096]{0:T(1024)} %get-tuple-element.164, f32[4096]{0:T(1024)S(1)} %get-tuple-element.153, f32[4,4096]{0,1:T(8,128)S(1)} %copy.270, f32[4096]{0:T(1024)S(1)} %fusion.83), kind=kCustom, calls=%fused_computation.59 | custom fusion | flops 49152 | bytes 2162736 | tf_op jit(solution)/shard_map/scatter-add | solution.py:76
  430.5 25.4 %scatter_custom_fusion.8 = f32[4,2051]{0,1:T(8,128)S(1)} fusion(f32[4,2051]{0,1:T(8,128)S(1)} %scatter_custom_fusion.7, s32[4096]{0:T(1024)} %get-tuple-element.165, f32[4096]{0:T(1024)S(1)} %get-tuple-element.152, f32[4,4096]{0,1:T(8,128)S(1)} %copy.270, f32[4096]{0:T(1024)S(1)} %fusion.83), kind=kCustom, calls=%fused_computation.57 | custom fusion | flops 49152 | bytes 2162736 | tf_op jit(solution)/shard_map/scatter-add | solution.py:76
  455.8 25.4 %scatter_custom_fusion.9 = f32[4,2051]{0,1:T(8,128)S(1)} fusion(f32[4,2051]{0,1:T(8,128)S(1)} %scatter_custom_fusion.8, s32[4096]{0:T(1024)} %copy-done.36, f32[4096]{0:T(1024)S(1)} %get-tuple-element.93, f32[4,4096]{0,1:T(8,128)S(1)} %copy.270, f32[4096]{0:T(1024)S(1)} %fusion.83), kind=kCustom, calls=%fused_computation.55 | custom fusion | flops 49152 | bytes 2162736 | tf_op jit(solution)/shard_map/scatter-add | solution.py:76
  487.6 36.2 %reduce-scatter.12.cloned.1.call-done = f32[256,4]{1,0:T(8,128)} async-done(((f32[2048,4]{1,0:T(8,128)}), f32[256,4]{1,0:T(8,128)}) %reduce-scatter.12.cloned.1.call-update) | async-done | bytes 4112
  550.6 37.0 %psum.74 = f32[]{:T(128)} all-reduce(f32[]{:T(128)} %get-tuple-element.71), channel_id=1, replica_groups=mesh['sky'=8,'tm'=4] {'sky','tm'}, use_global_device_ids=true, to_apply=%region_25.28 | all-reduce | flops 1 | bytes 8 | tf_op jit(solution)/shard_map/psum | solution.py:134
  631.1 14.1 %gather_fusion.9 = f32[4096,4]{1,0:T(8,128)} fusion(f32[4,2051]{0,1:T(8,128)S(1)} %copy.282, s32[4096]{0:T(1024)S(1)} %get-tuple-element.162), kind=kCustom, calls=%fused_computation.10.clone | custom fusion | bytes 147456 | tf_op jit(solution)/shard_map/jit(_take)/gather | solution.py:68
  659.2 14.1 %gather_fusion.7 = f32[4096,4]{1,0:T(8,128)} fusion(f32[4,2051]{0,1:T(8,128)S(1)} %copy.282, s32[4096]{0:T(1024)S(1)} %get-tuple-element.168), kind=kCustom, calls=%fused_computation.8.clone | custom fusion | bytes 147456 | tf_op jit(solution)/shard_map/jit(_take)/gather | solution.py:68
  699.0 22.8 %scatter_custom_fusion.10 = f32[5,1024]{0,1:T(8,128)S(1)} fusion(s32[4096]{0:T(1024)} %copy-done.35, f32[4096,5]{1,0:T(8,128)} %copy.286, f32[]{:T(128)} %constant.111.clone.1), kind=kCustom, calls=%fused_computation.109 | custom fusion | flops 20480 | bytes 20992 | tf_op jit(solution)/shard_map/scatter-add | solution.py:62
  722.0 15.8 %psum.77 = f32[5,1024]{1,0:T(8,128)S(1)} all-reduce(f32[5,1024]{1,0:T(8,128)S(1)} %copy.287), channel_id=1, replica_groups=mesh['sky'=8,'tm'=4] {'tm'}, use_global_device_ids=true, to_apply=%region_34.37 | all-reduce | flops 5120 | bytes 40960 | tf_op jit(solution)/shard_map/psum | solution.py:108
  739.1 14.1 %gather_fusion.10 = f32[4096,5]{1,0:T(8,128)} fusion(f32[5,1024]{0,1:T(8,128)S(1)} %copy.288, s32[4096]{0:T(1024)S(1)} %get-tuple-element.170), kind=kCustom, calls=%fused_computation.3.clone | custom fusion | bytes 180224 | tf_op jit(solution)/shard_map/jit(_take)/gather | solution.py:82
  755.5 25.3 %scatter_custom_fusion.11 = f32[4,2051]{0,1:T(8,128)S(1)} fusion(s32[4096]{0:T(1024)} %get-tuple-element.166, f32[4096]{0:T(1024)S(1)} %get-tuple-element.151, f32[]{:T(128)} %constant.111.clone.1, f32[4,4096]{0,1:T(8,128)S(1)} %copy.270, f32[4096]{0:T(1024)S(1)} %fusion.83), kind=kCustom, calls=%fused_computation.45 | custom fusion | flops 49152 | bytes 131632 | tf_op jit(solution)/shard_map/scatter-add | solution.py:76
  780.8 25.4 %scatter_custom_fusion.12 = f32[4,2051]{0,1:T(8,128)S(1)} fusion(f32[4,2051]{0,1:T(8,128)S(1)} %scatter_custom_fusion.11, s32[4096]{0:T(1024)} %get-tuple-element.164, f32[4096]{0:T(1024)S(1)} %get-tuple-element.150, f32[4,4096]{0,1:T(8,128)S(1)} %copy.270, f32[4096]{0:T(1024)S(1)} %fusion.83), kind=kCustom, calls=%fused_computation.43 | custom fusion | flops 49152 | bytes 2162736 | tf_op jit(solution)/shard_map/scatter-add | solution.py:76
  806.2 25.4 %scatter_custom_fusion.13 = f32[4,2051]{0,1:T(8,128)S(1)} fusion(f32[4,2051]{0,1:T(8,128)S(1)} %scatter_custom_fusion.12, s32[4096]{0:T(1024)} %get-tuple-element.165, f32[4096]{0:T(1024)S(1)} %get-tuple-element.149, f32[4,4096]{0,1:T(8,128)S(1)} %copy.270, f32[4096]{0:T(1024)S(1)} %fusion.83), kind=kCustom, calls=%fused_computation.41 | custom fusion | flops 49152 | bytes 2162736 | tf_op jit(solution)/shard_map/scatter-add | solution.py:76
  831.6 25.6 %scatter_custom_fusion.14 = f32[4,2051]{0,1:T(8,128)S(1)} fusion(f32[4,2051]{0,1:T(8,128)S(1)} %scatter_custom_fusion.13, s32[4096]{0:T(1024)} %copy-done.36, f32[4096]{0:T(1024)S(1)} %get-tuple-element.82, f32[4,4096]{0,1:T(8,128)S(1)} %copy.270, f32[4096]{0:T(1024)S(1)} %fusion.83), kind=kCustom, calls=%fused_computation.39 | custom fusion | flops 49152 | bytes 2162736 | tf_op jit(solution)/shard_map/scatter-add | solution.py:76
  863.4 36.8 %reduce-scatter.14.cloned.1.call-done = f32[256,4]{1,0:T(8,128)} async-done(((f32[2048,4]{1,0:T(8,128)}), f32[256,4]{1,0:T(8,128)}) %reduce-scatter.14.cloned.1.call-update) | async-done | bytes 4112
  901.8 39.5 %psum.78 = f32[]{:T(128)} all-reduce(f32[]{:T(128)} %multiply_reduce_fusion), channel_id=1, replica_groups=mesh['sky'=8,'tm'=4] {'sky','tm'}, use_global_device_ids=true, to_apply=%region_42.45 | all-reduce | flops 1 | bytes 8 | tf_op jit(solution)/shard_map/psum | solution.py:134
  987.9 14.1 %gather_fusion.12 = f32[4096,4]{1,0:T(8,128)} fusion(f32[4,2051]{0,1:T(8,128)S(1)} %copy.291, s32[4096]{0:T(1024)S(1)} %get-tuple-element.168), kind=kCustom, calls=%fused_computation.12.clone | custom fusion | bytes 147456 | tf_op jit(solution)/shard_map/jit(_take)/gather | solution.py:68
  1025.8 22.6 %scatter_custom_fusion.15 = f32[5,1024]{0,1:T(8,128)S(1)} fusion(s32[4096]{0:T(1024)} %copy-done.35, f32[4096,5]{1,0:T(8,128)S(1)} %copy.295, f32[]{:T(128)} %constant.111.clone.1), kind=kCustom, calls=%fused_computation.107 | custom fusion | flops 20480 | bytes 20992 | tf_op jit(solution)/shard_map/scatter-add | solution.py:62
  1048.6 17.1 %psum.79 = f32[5,1024]{1,0:T(8,128)S(1)} all-reduce(f32[5,1024]{1,0:T(8,128)S(1)} %copy.296), channel_id=1, replica_groups=mesh['sky'=8,'tm'=4] {'tm'}, use_global_device_ids=true, to_apply=%region_48.51 | all-reduce | flops 5120 | bytes 40960 | tf_op jit(solution)/shard_map/psum | solution.py:108
  (196 shorter events, 289.2 us)
Async XLA Ops:
  7.2 65.2 %all-reduce.2.cloned.1.call-start = ((), (), s32[]{:S(2)}) async-start(), calls=%async_computation.3 | async-start | bytes 196608 | tf_op jit(solution)/shard_map/psum | solution.py:101
  11.7 60.7 %copy-start.34 = (f32[5,1024]{1,0:T(8,128)S(1)}, f32[5,1024]{1,0:T(8,128)}, u32[]{:S(2)}) copy-start(f32[5,1024]{1,0:T(8,128)} %param.25) | copy-start | bytes 61444
  35.0 202.8 %reduce-scatter.10.cloned.1.call-start = ((), (), s32[]{:S(2)}) async-start(), calls=%async_computation.4 | async-start | bytes 1179648
  35.7 132.3 %copy-start.36 = (s32[4096]{0:T(1024)}, s32[4096]{0:T(1024)S(1)}, u32[]{:S(2)}) copy-start(s32[4096]{0:T(1024)S(1)} %get-tuple-element.169) | copy-start | bytes 49156
  35.7 343.7 %copy-start.21 = (pred[4096]{0:T(1024)(128)(4,1)}, pred[4096]{0:T(1024)(128)(4,1)S(1)}, u32[]{:S(2)}) copy-start(pred[4096]{0:T(1024)(128)(4,1)S(1)} %compare_and_fusion.4) | copy-start | bytes 12292
  73.6 288.4 %copy-start.3 = (f32[1,1024]{1,0:T(1,128)}, f32[1,1024]{1,0:T(1,128)S(1)}, u32[]{:S(2)}) copy-start(f32[1,1024]{1,0:T(1,128)S(1)} %get-tuple-element.126) | copy-start | bytes 12292
  73.6 288.4 %copy-start.5 = (f32[1,1024]{1,0:T(1,128)}, f32[1,1024]{1,0:T(1,128)S(1)}, u32[]{:S(2)}) copy-start(f32[1,1024]{1,0:T(1,128)S(1)} %get-tuple-element.127) | copy-start | bytes 12292
  73.6 288.4 %copy-start.7 = (f32[1,1024]{1,0:T(1,128)}, f32[1,1024]{1,0:T(1,128)S(1)}, u32[]{:S(2)}) copy-start(f32[1,1024]{1,0:T(1,128)S(1)} %get-tuple-element.128) | copy-start | bytes 12292
  194.6 4.6 collective-permute-start
  201.2 322.6 %reduce-scatter.12.cloned.1.call-start = ((), (), s32[]{:S(2)}) async-start(), calls=%async_computation.5 | async-start | bytes 1179648
  201.3 109.3 %copy-start.13 = (pred[4096]{0:T(1024)(128)(4,1)}, pred[4096]{0:T(1024)(128)(4,1)S(1)}, u32[]{:S(2)}) copy-start(pred[4096]{0:T(1024)(128)(4,1)S(1)} %get-tuple-element.158) | copy-start | bytes 12292
  201.3 109.3 %copy-start.15 = (pred[4096]{0:T(1024)(128)(4,1)}, pred[4096]{0:T(1024)(128)(4,1)S(1)}, u32[]{:S(2)}) copy-start(pred[4096]{0:T(1024)(128)(4,1)S(1)} %get-tuple-element.159) | copy-start | bytes 12292
  201.3 109.3 %copy-start.17 = (pred[4096]{0:T(1024)(128)(4,1)}, pred[4096]{0:T(1024)(128)(4,1)S(1)}, u32[]{:S(2)}) copy-start(pred[4096]{0:T(1024)(128)(4,1)S(1)} %get-tuple-element.160) | copy-start | bytes 12292
  201.3 109.3 %copy-start.19 = (pred[4096]{0:T(1024)(128)(4,1)}, pred[4096]{0:T(1024)(128)(4,1)S(1)}, u32[]{:S(2)}) copy-start(pred[4096]{0:T(1024)(128)(4,1)S(1)} %get-tuple-element.161) | copy-start | bytes 12292
  248.8 5.5 collective-permute-start.1
  319.6 42.4 %copy-start.26 = (f32[1,1024]{1,0:T(1,128)S(1)}, f32[1,1024]{1,0:T(1,128)}, u32[]{:S(2)}) copy-start(f32[1,1024]{1,0:T(1,128)} %get-tuple-element.111) | copy-start | bytes 12292
  319.6 42.4 %copy-start.28 = (f32[1,1024]{1,0:T(1,128)S(1)}, f32[1,1024]{1,0:T(1,128)}, u32[]{:S(2)}) copy-start(f32[1,1024]{1,0:T(1,128)} %get-tuple-element.112) | copy-start | bytes 12292
  319.6 42.4 %copy-start.30 = (f32[1,1024]{1,0:T(1,128)S(1)}, f32[1,1024]{1,0:T(1,128)}, u32[]{:S(2)}) copy-start(f32[1,1024]{1,0:T(1,128)} %get-tuple-element.113) | copy-start | bytes 12292
  319.6 42.4 %copy-start.32 = (f32[1,1024]{1,0:T(1,128)S(1)}, f32[1,1024]{1,0:T(1,128)}, u32[]{:S(2)}) copy-start(f32[1,1024]{1,0:T(1,128)} %get-tuple-element.114) | copy-start | bytes 12292
  482.3 2.6 collective-permute-start.2
  487.5 412.7 %reduce-scatter.14.cloned.1.call-start = ((), (), s32[]{:S(2)}) async-start(), calls=%async_computation.6 | async-start | bytes 1179648
  487.6 143.0 %copy-start.11 = (f32[4,256]{1,0:T(4,128)}, f32[4,256]{1,0:T(4,128)S(1)}, u32[]{:S(2)}) copy-start(f32[4,256]{1,0:T(4,128)S(1)} %copy.300) | copy-start | bytes 12292
  625.2 5.5 collective-permute-start.3
  696.9 41.0 %copy-start.27 = (f32[1,1024]{1,0:T(1,128)S(1)}, f32[1,1024]{1,0:T(1,128)}, u32[]{:S(2)}) copy-start(f32[1,1024]{1,0:T(1,128)} %get-tuple-element.111) | copy-start | bytes 12292
  696.9 41.0 %copy-start.29 = (f32[1,1024]{1,0:T(1,128)S(1)}, f32[1,1024]{1,0:T(1,128)}, u32[]{:S(2)}) copy-start(f32[1,1024]{1,0:T(1,128)} %get-tuple-element.112) | copy-start | bytes 12292
  857.2 85.5 %copy-start.12 = (f32[4,256]{1,0:T(4,128)S(1)}, f32[4,256]{1,0:T(4,128)}, u32[]{:S(2)}) copy-start(f32[4,256]{1,0:T(4,128)} %copy-done.11) | copy-start | bytes 12292
  858.2 3.2 collective-permute-start.4
  863.4 152.7 %copy-start.14 = (pred[4096]{0:T(1024)(128)(4,1)S(1)}, pred[4096]{0:T(1024)(128)(4,1)}, u32[]{:S(2)}) copy-start(pred[4096]{0:T(1024)(128)(4,1)} %copy-done.13) | copy-start | bytes 12292
  863.4 152.7 %copy-start.16 = (pred[4096]{0:T(1024)(128)(4,1)S(1)}, pred[4096]{0:T(1024)(128)(4,1)}, u32[]{:S(2)}) copy-start(pred[4096]{0:T(1024)(128)(4,1)} %copy-done.15) | copy-start | bytes 12292
  863.4 152.7 %copy-start.18 = (pred[4096]{0:T(1024)(128)(4,1)S(1)}, pred[4096]{0:T(1024)(128)(4,1)}, u32[]{:S(2)}) copy-start(pred[4096]{0:T(1024)(128)(4,1)} %copy-done.17) | copy-start | bytes 12292
  863.4 152.7 %copy-start.20 = (pred[4096]{0:T(1024)(128)(4,1)S(1)}, pred[4096]{0:T(1024)(128)(4,1)}, u32[]{:S(2)}) copy-start(pred[4096]{0:T(1024)(128)(4,1)} %copy-done.19) | copy-start | bytes 12292
  953.9 5.5 collective-permute-start.5
  (15 other events, 388.3 us)
Sparse Core Ops, SparseCore 0:
  35.1 37.1 all-reduce.1
  201.3 36.4 reduce-scatter.9
  487.6 36.1 reduce-scatter.11
  863.5 36.6 reduce-scatter.13
